TPU v7x, 128 devices: a whole 4x4x4 slice. The times are simulated.
128 devices in a mesh: dp: 8 (over y, x_lo), tp: 16 (over z, x_hi, core).
Axes of the slice: x: 4 (x_hi: 2, x_lo: 2; x = x_hi * 2 + x_lo), y: 4, z: 4, core: 2. Of those that a mesh axis runs over, the one named last changes fastest.
Arguments:
- gradients: bfloat16 [8, 4, 3072, 768], P('dp', None, 'tp'), may hold values from -6 to 6, as said below
- right_factor: float32 [4, 768, 8], replicated, may hold values from -6 to 6
- weights_before: float32 [4, 3072, 768], P(None, 'tp', 'dp'), may hold values from -0.21875 to 0.21875
- momentum: float32 [4, 3072, 768], P(None, 'tp', 'dp'), may hold values from -0.3125 to 0.3125
Outputs:
- new_weights: float32 [4, 3072, 768], P(None, 'tp', 'dp')
- new_basis: float32 [4, 768, 8], replicated
- new_momentum: float32 [4, 3072, 768], P(None, 'tp', 'dp')
Inputs may be any that keep to these rules, and one draw needn't show every extreme that they name: gradients holds numbers from -6 to 6.
All inputs are finite; a program needn't handle non-finite values.
Results may differ from a plain program's by a relative error of at most 0.0003.
Values sent between devices are 32-bit elements.
A program may use at most 64 MiB of HBM per device.

v0:
```python
import jax
import jax.numpy as jnp
from jax import lax
from jax.sharding import Mesh
from jax.sharding import PartitionSpec as P

RANK = 8
DP = ("dp_0", "dp_1")
DP_TP = ("dp_0", "dp_1", "tp")


def by_axis(x, axes):
    for axis in axes:
        x = lax.psum(x, axis)
    return x


def on_device(gradients, right_factor, weights_before, momentum):
    own_grads = gradients[0]
    part_left = jnp.einsum(
        "liw,lwr->lir",
        own_grads,
        right_factor.astype(jnp.bfloat16),
        preferred_element_type=jnp.float32,
    )
    left = by_axis(part_left, DP)
    part_gram = jnp.einsum("lir,lis->lrs", left, left, precision=lax.Precision.HIGHEST)
    small_left = left.astype(jnp.bfloat16)
    part_right = jnp.einsum(
        "liw,lir->lwr", own_grads, small_left, preferred_element_type=jnp.float32
    )
    own_share = part_gram / lax.axis_size(DP)
    right, gram = lax.psum((part_right, own_share), DP_TP)
    gram = gram + 0.001 * jnp.mean(jnp.diagonal(gram, axis1=1, axis2=2), axis=1)[
        :, None, None
    ] * jnp.eye(RANK, dtype=jnp.float32)
    place = lax.axis_index(DP) * weights_before.shape[2]
    own_right = lax.dynamic_slice_in_dim(right, place, weights_before.shape[2], axis=1)
    root = jnp.linalg.cholesky(gram)
    half = lax.linalg.triangular_solve(
        root, jnp.swapaxes(own_right, 1, 2), left_side=True, lower=True
    )
    mixed = lax.linalg.triangular_solve(root, half, left_side=True, lower=True, transpose_a=True)
    change = jnp.einsum(
        "lir,lrw->liw", left, mixed, precision=lax.Precision.HIGHEST
    ) / lax.axis_size(DP)
    new_momentum = 0.9 * momentum + change
    new_weights = weights_before - 0.02 * new_momentum
    new_basis = right * lax.rsqrt(jnp.mean(right * right, axis=(1, 2), keepdims=True) + 1e-12)
    return (new_weights, new_basis, new_momentum)


def solution(mesh):
    split = Mesh(mesh.devices.reshape(4, 2, mesh.shape["tp"]), ("dp_0", "dp_1", "tp"))
    in_specs = (P(DP, None, "tp", None), P(), P(None, "tp", DP), P(None, "tp", DP))
    out_specs = (P(None, "tp", DP), P(), P(None, "tp", DP))
    return jax.shard_map(
        on_device, mesh=split, in_specs=in_specs, out_specs=out_specs, check_vma=False
    )
```

profile of v0, /device:TPU:1, one launch (start us, length us, event | category | flops | bytes accessed | tf_op | source)
XLA Modules:
  0.0 195.7 jit_solution(8125592697090335394)
XLA Ops:
  7.2 1.2 copy-done
  8.4 1.3 fusion.3
  9.7 14.5 %psum.28 = f32[4,192,8]{1,2,0:T(8,128)S(1)} all-reduce(f32[4,192,8]{1,2,0:T(8,128)S(1)} %fusion.3), channel_id=1, replica_groups=mesh['dp_0'=4,'dp_1'=2,'tp'=16] {'dp_0'}, use_global_device_ids=true, to_apply=%region_0.0 | all-reduce | flops 6144 | bytes 49152 | tf_op jit(solution)/shard_map/psum | solution.py:14
  24.3 6.4 %psum.29 = f32[4,192,8]{1,2,0:T(8,128)S(1)} all-reduce(f32[4,192,8]{1,2,0:T(8,128)S(1)} %psum.28), channel_id=1, replica_groups=mesh['dp_0'=4,'dp_1'=2,'tp'=16] {'dp_1'}, use_global_device_ids=true, to_apply=%region_1.0 | all-reduce | flops 6144 | bytes 49152 | tf_op jit(solution)/shard_map/psum | solution.py:14
  30.6 0.9 fusion.5
  31.6 0.2 convolution_multiply_fusion.1
  31.8 0.1 copy.13
  31.9 71.2 %psum.30 = f32[4,8,8]{1,2,0:T(8,128)S(1)} all-reduce(f32[4,8,8]{1,2,0:T(8,128)S(1)} %convolution_multiply_fusion.1), channel_id=1, replica_groups=mesh['dp_0'=4,'dp_1'=2,'tp'=16] {'dp_0','dp_1','tp'}, use_global_device_ids=true, to_apply=%region_2.0 | all-reduce | flops 256 | bytes 2048 | tf_op jit(solution)/shard_map/psum | solution.py:33
  103.1 0.1 copy.12
  103.2 0.6 gather_fusion
  103.8 0.1 multiply_add_fusion
  103.9 0.1 copy.14
  104.0 0.1 fusion.13
  104.0 2.9 %custom-call.9 = f32[4,8,8]{2,1,0:T(8,128)S(1)} custom-call(f32[4,8,8]{2,1,0:T(8,128)S(1)} %fusion.13), custom_call_target="Cholesky" | custom-call | tf_op jit(solution)/shard_map/jit(cholesky)/cholesky | solution.py:39
  106.9 0.1 select_reduce_fusion
  107.0 0.1 compare_reduce_fusion
  107.1 0.1 select_bitcast_fusion
  107.2 2.5 %custom-call.10 = f32[4,1,8,8]{2,3,1,0:T(8,128)S(1)} custom-call(f32[4,1,8,8]{3,2,1,0:T(8,128)S(1)} %select_bitcast_fusion), custom_call_target="InvertDiagBlocksLowerTriangular" | custom-call | tf_op jit(solution)/shard_map/triangular_solve | solution.py:43
  109.7 74.4 %all-reduce.2.cloned.1.call-done = f32[4,768,8]{1,2,0:T(8,128)} async-done(((f32[4,768,8]{1,2,0:T(8,128)}), f32[4,768,8]{1,2,0:T(8,128)}) %all-reduce.2.cloned.1.call-update) | async-done | bytes 98320 | tf_op jit(solution)/shard_map/psum | solution.py:33
  184.1 1.1 multiply_reduce_fusion
  185.2 1.0 fusion.11
  186.2 0.2 fusion.9
  186.4 1.7 multiply_subtract_fusion
  188.1 0.7 broadcast_multiply_fusion
  (16 shorter events, 0.1 us)
Async XLA Ops:
  7.2 1.3 copy-start
  7.2 176.9 %all-reduce.2.cloned.1.call-start = ((), (), s32[]{:S(2)}) async-start(), calls=%async_computation | async-start | bytes 196608 | tf_op jit(solution)/shard_map/psum | solution.py:33
  9.7 176.7 %copy-start.2 = (f32[4,192,96]{2,1,0:T(8,128)S(1)}, f32[4,192,96]{2,1,0:T(8,128)}, u32[]{:S(2)}) copy-start(f32[4,192,96]{2,1,0:T(8,128)} %param.6) | copy-start | bytes 884740
  9.7 176.7 %copy-start.3 = (f32[4,192,96]{2,1,0:T(8,128)S(1)}, f32[4,192,96]{2,1,0:T(8,128)}, u32[]{:S(2)}) copy-start(f32[4,192,96]{2,1,0:T(8,128)} %param.7) | copy-start | bytes 884740
  184.1 4.0 %copy-start.1 = (f32[4,768,8]{1,2,0:T(8,128)S(1)}, f32[4,768,8]{1,2,0:T(8,128)}, u32[]{:S(2)}) copy-start(f32[4,768,8]{1,2,0:T(8,128)} %all-reduce.2.cloned.1.call-done) | copy-start | bytes 294916
Sparse Core Ops, SparseCore 0:
  31.7 152.3 all-reduce.1
where the time goes:
time: 196 us
  blocking collectives  92.1 us (47%)
  waiting for transfers between devices  74.4 us (38%)
  between operations  14.1 us (7%)
  other arithmetic  7.66 us (4%)
  matrix products  5.23 us (3%)
  local copies, waits for them, and re-layouts  2.08 us (1%)
    psum x1, waiting for transfers between devices, on_device(): right, gram = lax.psum((part_right, own_share), DP_TP)  74.4 us
    psum x1, blocking collectives, on_device(): right, gram = lax.psum((part_right, own_share), DP_TP)  71.2 us
    psum x2, blocking collectives, by_axis(): x = lax.psum(x, axis)  20.9 us
  transfers between devices with their start and end apart: 1, of which 1 were waited for; matrix products, arithmetic and copies ran while one was open for 4% of the time, Pallas kernels for 0%

commit v1 on v0

v1 whole, which is shorter than its diff:
```python
import functools

import jax
import jax.numpy as jnp
from jax import lax
from jax.experimental import pallas as pl
from jax.experimental.pallas import tpu as pltpu
from jax.sharding import PartitionSpec as P

RANK = 8
LANES = 128
MESH = pl.DeviceIdType.MESH
F32 = jnp.float32
BF16 = jnp.bfloat16


def remote(src, dst, send_sem, recv_sem, dp, tp):
    return pltpu.make_async_remote_copy(
        src_ref=src,
        dst_ref=dst,
        send_sem=send_sem,
        recv_sem=recv_sem,
        device_id=(dp, tp),
        device_id_type=MESH,
    )


def take_bytes(ref, sem):
    pltpu.make_async_copy(ref, ref, sem).wait()


def split3(value):
    high = value.astype(BF16).astype(F32)
    rest = value - high
    middle = rest.astype(BF16).astype(F32)
    return high, middle, rest - middle


def kernel(
    n_dp,
    n_far,
    grads_hbm,
    factor_ref,
    weights_hbm,
    momentum_hbm,
    new_weights_ref,
    new_basis_ref,
    new_momentum_ref,
    grads,
    weights,
    momentum,
    lefts,
    pieces,
    parts,
    sums,
    whole,
    turned,
    load_sems,
    send_sems,
    recv_sems,
):
    layers, rows, width = grads.shape
    cols = width // n_dp
    half = layers // 2
    dp = lax.axis_index("dp")
    tp = lax.axis_index("tp")
    core = lax.rem(tp, 2)
    far = tp // 2
    group = dp * 2 + core

    def dp_peer(k):
        return lax.rem(dp + k, n_dp)

    def far_peer(k):
        return lax.rem(far + k, n_far)

    barrier = pltpu.get_barrier_semaphore()

    def greet(to_dp, to_tp):
        pl.semaphore_signal(barrier, inc=1, device_id=(to_dp, to_tp), device_id_type=MESH)

    other = far * 2 + (1 - core)
    for k in range(1, n_far):
        greet(dp, far_peer(k) * 2 + core)
    for k in range(1, n_dp):
        greet(dp_peer(k), tp)
        greet(dp_peer(k), other)
    greet(dp, other)

    loads = [
        pltpu.make_async_copy(grads_hbm.at[l], grads.at[l], load_sems.at[l]) for l in range(layers)
    ]
    late = [
        pltpu.make_async_copy(weights_hbm, weights, load_sems.at[layers]),
        pltpu.make_async_copy(momentum_hbm, momentum, load_sems.at[layers + 1]),
    ]
    for load in loads + late:
        load.start()

    left_parts = []
    for l in range(layers):
        loads[l].wait()
        left_parts.append(
            lax.dot_general(
                factor_ref[l].astype(BF16),
                grads[l],
                (((1,), (1,)), ((), ())),
                preferred_element_type=F32,
            )
        )
    for l in range(layers):
        lefts[dp, l] = left_parts[l][:, :LANES]
    for h in range(half):
        lefts[dp, layers + h] = jnp.concatenate(
            [left_parts[2 * h][:, LANES:], left_parts[2 * h + 1][:, LANES:]], axis=1
        )

    pl.semaphore_wait(barrier, n_far - 1 + 2 * n_dp - 1)

    copies_a = [
        remote(lefts.at[dp], lefts.at[dp], send_sems.at[0], recv_sems.at[0], dp_peer(k), tp)
        for k in range(1, n_dp)
    ]
    for copy in copies_a:
        copy.start()
    take_bytes(lefts.at[pl.ds(0, n_dp - 1)], recv_sems.at[0])

    total = lefts[0]
    for k in range(1, n_dp):
        total = total + lefts[k]
    rest = rows - LANES
    left = []
    for l in range(layers):
        tail = total[layers + l // 2][:, (l % 2) * rest : (l % 2 + 1) * rest]
        left.append(jnp.concatenate([total[l], tail], axis=1))

    for l in range(layers):
        right = jnp.dot(left[l].astype(BF16), grads[l], preferred_element_type=F32)
        gram = lax.dot_general(
            left[l],
            left[l],
            (((1,), (1,)), ((), ())),
            precision=lax.Precision.HIGHEST,
            preferred_element_type=F32,
        ) * (1.0 / n_dp)
        spare = jnp.concatenate(
            [gram, jnp.zeros((RANK, LANES - cols - RANK), F32)], axis=1
        )
        for d in range(n_dp):
            pieces[d * 2 + l // half, l % half] = jnp.concatenate(
                [right[:, d * cols : (d + 1) * cols], spare], axis=1
            )

    copies_1 = []
    for k in range(n_dp):
        for side in range(2):
            if k == 0 and side == 0:
                continue
            to_core = core if side == 0 else 1 - core
            to_dp = dp_peer(k)
            copies_1.append(
                remote(
                    pieces.at[to_dp * 2 + to_core],
                    parts.at[group],
                    send_sems.at[1],
                    recv_sems.at[1],
                    to_dp,
                    far * 2 + to_core,
                )
            )
    for copy in copies_1:
        copy.start()
    parts[group] = pieces[group]

    for l in range(layers):
        high, middle, low = split3(left[l])
        turned[l] = jnp.concatenate(
            [high, high, middle, high, middle, low], axis=0
        ).T.astype(BF16)

    n_group = 2 * n_dp
    take_bytes(parts.at[pl.ds(0, n_group - 1)], recv_sems.at[1])
    own = parts[0]
    for k in range(1, n_group):
        own = own + parts[k]
    sums[far] = own

    copies_2 = [
        remote(
            sums.at[far], sums.at[far], send_sems.at[2], recv_sems.at[2], dp, far_peer(k) * 2 + core
        )
        for k in range(1, n_far)
    ]
    for copy in copies_2:
        copy.start()
    take_bytes(sums.at[pl.ds(0, n_far - 1)], recv_sems.at[2])
    own = sums[0]
    for k in range(1, n_far):
        own = own + sums[k]
    whole[group] = own

    near = remote(
        whole.at[group], whole.at[group], send_sems.at[3], recv_sems.at[3], dp, other
    )
    near.start()
    copies_3 = []
    for k in range(1, n_dp):
        for to_tp in (tp, other):
            copies_3.append(
                remote(
                    whole.at[group],
                    whole.at[group],
                    send_sems.at[4],
                    recv_sems.at[4],
                    dp_peer(k),
                    to_tp,
                )
            )
    for copy in copies_3:
        copy.start()

    near.wait_recv()
    tile = jnp.concatenate([whole[dp * 2], whole[dp * 2 + 1]], axis=0)
    row = lax.broadcasted_iota(jnp.int32, tile.shape, 1)
    lane = lax.broadcasted_iota(jnp.int32, tile.shape, 2)
    diagonal = lane == row + cols
    trace = jnp.sum(jnp.where(diagonal, tile, 0.0), axis=(1, 2), keepdims=True)
    tile = tile + jnp.where(diagonal, trace * (0.001 / RANK), 0.0)
    for k in range(RANK):
        pivot_row = tile[:, k : k + 1, :] / tile[:, k : k + 1, cols + k : cols + k + 1]
        column = tile[:, :, cols + k : cols + k + 1]
        tile = jnp.where(row == k, pivot_row, tile - column * pivot_row)
    mixed = tile * (1.0 / n_dp)

    for load in late:
        load.wait()
    for l in range(layers):
        high, middle, low = split3(mixed[l])
        stack = jnp.concatenate([high, middle, high, low, middle, high], axis=0).astype(BF16)
        change = jnp.dot(turned[l], stack, preferred_element_type=F32)[:, :cols]
        moved = 0.9 * momentum[l] + change
        new_momentum_ref[l] = moved
        new_weights_ref[l] = weights[l] - 0.02 * moved

    take_bytes(whole.at[pl.ds(0, n_group - 2)], recv_sems.at[4])
    for l in range(layers):
        right = jnp.concatenate(
            [whole[d * 2 + l // half, l % half][:, :cols] for d in range(n_dp)], axis=1
        )
        mean = jnp.sum(right * right, axis=(0, 1), keepdims=True) * (1.0 / (RANK * width))
        new_basis_ref[l] = right * lax.rsqrt(mean + 1e-12)

    take_bytes(lefts.at[pl.ds(0, n_dp - 1)], send_sems.at[0])
    take_bytes(parts.at[pl.ds(0, n_group - 1)], send_sems.at[1])
    take_bytes(sums.at[pl.ds(0, n_far - 1)], send_sems.at[2])
    near.wait_send()
    take_bytes(whole.at[pl.ds(0, n_group - 2)], send_sems.at[4])


def solution(mesh):
    n_dp = mesh.shape["dp"]
    n_far = mesh.shape["tp"] // 2

    def step(gradients, right_factor, weights_before, momentum):
        grads = gradients[0]
        factor = jnp.swapaxes(right_factor, 1, 2)
        layers, rows, width = grads.shape
        half = layers // 2
        block = weights_before.shape
        vmem = pl.BlockSpec(memory_space=pltpu.VMEM)
        hbm = pl.BlockSpec(memory_space=pl.ANY)
        tile = (half, RANK, LANES)
        new_weights, new_basis, new_momentum = pl.pallas_call(
            functools.partial(kernel, n_dp, n_far),
            out_shape=(
                jax.ShapeDtypeStruct(block, F32),
                jax.ShapeDtypeStruct(factor.shape, F32),
                jax.ShapeDtypeStruct(block, F32),
            ),
            in_specs=[hbm, vmem, hbm, hbm],
            out_specs=(vmem, vmem, vmem),
            scratch_shapes=[
                pltpu.VMEM(grads.shape, BF16),
                pltpu.VMEM(block, F32),
                pltpu.VMEM(block, F32),
                pltpu.VMEM((n_dp, layers + half, RANK, LANES), F32),
                pltpu.VMEM((2 * n_dp,) + tile, F32),
                pltpu.VMEM((2 * n_dp,) + tile, F32),
                pltpu.VMEM((n_far,) + tile, F32),
                pltpu.VMEM((2 * n_dp,) + tile, F32),
                pltpu.VMEM((layers, rows, 6 * RANK), BF16),
                pltpu.SemaphoreType.DMA((layers + 2,)),
                pltpu.SemaphoreType.DMA((5,)),
                pltpu.SemaphoreType.DMA((5,)),
            ],
            compiler_params=pltpu.CompilerParams(collective_id=0, has_side_effects=True),
        )(grads, factor, weights_before, momentum)
        return new_weights, jnp.swapaxes(new_basis, 1, 2), new_momentum

    return jax.shard_map(
        step,
        mesh=mesh,
        in_specs=(P("dp", None, "tp", None), P(), P(None, "tp", "dp"), P(None, "tp", "dp")),
        out_specs=(P(None, "tp", "dp"), P(), P(None, "tp", "dp")),
        check_vma=False,
    )
```

time: 196 us -> 33.2 us (0.17)
  blocking collectives: 92.1 us -> 0 us
  waiting for transfers between devices: 74.4 us -> 0 us
  Pallas kernels: 0 us -> 28.2 us
  between operations: 14.1 us -> 0.65 us
  other arithmetic: 7.66 us -> 0 us
  matrix products: 5.23 us -> 0 us
  local copies, waits for them, and re-layouts: 2.08 us -> 4.11 us
    psum x3 -> x0, blocking collectives: 92.1 us -> none  [the longest x1 71.2 us: on_device(): right, gram = lax.psum((part_right, own_share), DP_TP)]
    psum x1 -> x0, waiting for transfers between devices: 74.4 us -> none  [on_device(): right, gram = lax.psum((part_right, own_share), DP_TP)]
    pallas_call x0 -> x1, Pallas kernels: none -> 28.2 us  [step(): pl.pallas_call(functools.partial(kernel, n_dp, n_far), out_shape=(jax.Sha...]
    another operation x7 -> x0, other arithmetic: 5.67 us -> none  [the longest x4 3.08 us: on_device(): root = jnp.linalg.cholesky(gram)]
    dot_general x4 -> x0, matrix products: 4.05 us -> none  [the longest x1 1.7 us: on_device(): jnp.einsum('lir,lrw->liw', left, mixed, precision=lax.Precision.HIGHEST)]
    unnamed x8 -> x5, local copies, waits for them, and re-layouts: 1.24 us -> 4.11 us
  transfers between devices with their start and end apart: 1 -> 0, of which waited for: 1 -> 0; matrix products, arithmetic and copies ran while one was open for 4% -> 0% of each run, Pallas kernels for 0% -> 0%
where the time goes in v1:
time: 33.2 us; the launch traced here: 33 us
  Pallas kernels  28.2 us (85%)
  local copies, waits for them, and re-layouts  4.11 us (12%)
  between operations  0.65 us (2%)
    pallas_call x1, Pallas kernels, step(): pl.pallas_call(functools.partial(kernel, n_dp, n_far), out_shape=(jax.Sha...  28.2 us
    unnamed x5, local copies, waits for them, and re-layouts  4.11 us

profile of v1, /device:TPU:1, one launch (start us, length us, event | category | flops | bytes accessed | tf_op | source)
XLA Modules:
  0.0 33.0 jit_solution(7593162784134856216)
XLA Ops:
  0.6 28.2 %shard_map.67 = (f32[4,192,96]{2,1,0:T(8,128)}, f32[4,8,768]{2,1,0:T(8,128)}, f32[4,192,96]{2,1,0:T(8,128)}) custom-call(bf16[4,192,768]{2,1,0:T(8,128)(2,1)} %bitcast.3, f32[4,8,768]{2,1,0:T(8,128)} %bitcast.4, f32[4,192,96]{2,1,0:T(8,128)} %weights_hbm.1, f32[4,192,96]{2,1,0:T(8,128)} %momentum_hbm.1), custom_call_target="tpu_custom_call" | custom-call | tf_op jit(solution)/shard_map/pallas_call | solution.py:273
  28.8 0.0 copy-start
  28.9 1.8 %copy.10 = f32[4,192,96]{2,1,0:T(8,128)} copy(f32[4,192,96]{2,1,0:T(8,128)} %get-tuple-element.12) | data formatting | bytes 589824
  30.7 1.5 %copy.11 = f32[4,768,8]{1,2,0:T(8,128)} copy(f32[4,768,8]{1,2,0:T(8,128)} %bitcast.5) | data formatting | bytes 196608
  32.2 0.0 copy-done
  32.2 0.7 %copy.12 = f32[4,192,96]{2,1,0:T(8,128)} copy(f32[4,192,96]{2,1,0:T(8,128)S(1)} %copy-done) | data formatting | bytes 589824
Async XLA Ops:
  28.8 3.4 %copy-start = (f32[4,192,96]{2,1,0:T(8,128)S(1)}, f32[4,192,96]{2,1,0:T(8,128)}, u32[]{:S(2)}) copy-start(f32[4,192,96]{2,1,0:T(8,128)} %get-tuple-element.14) | copy-start | bytes 884740

commit v2 on v1

--- a/solution.py
+++ b/solution.py
@@ -29,6 +29,14 @@
     pltpu.make_async_copy(ref, ref, sem).wait()
 
 
+def farthest(ring, step):
+    def hops(offset):
+        return min(offset[0], ring - offset[0]) + step * offset[1]
+
+    offsets = [(up, over) for up in range(ring) for over in range(2) if up or over]
+    return sorted(offsets, key=hops, reverse=True)
+
+
 def split3(value):
     high = value.astype(BF16).astype(F32)
     rest = value - high
@@ -40,13 +48,14 @@
     n_dp,
     n_far,
     grads_hbm,
-    factor_ref,
+    factor_hbm,
     weights_hbm,
     momentum_hbm,
     new_weights_ref,
     new_basis_ref,
     new_momentum_ref,
     grads,
+    factor,
     weights,
     momentum,
     lefts,
@@ -68,11 +77,14 @@
     far = tp // 2
     group = dp * 2 + core
 
-    def dp_peer(k):
-        return lax.rem(dp + k, n_dp)
-
-    def far_peer(k):
-        return lax.rem(far + k, n_far)
+    dp_peers = [
+        lax.rem(dp // 2 + up, n_dp // 2) * 2 + lax.rem(dp + over, 2)
+        for up, over in farthest(n_dp // 2, 1)
+    ]
+    far_peers = [
+        lax.rem(far // 2 + up, n_far // 2) * 2 + lax.rem(far + over, 2)
+        for up, over in farthest(n_far // 2, 2)
+    ]
 
     barrier = pltpu.get_barrier_semaphore()
 
@@ -80,11 +92,11 @@
         pl.semaphore_signal(barrier, inc=1, device_id=(to_dp, to_tp), device_id_type=MESH)
 
     other = far * 2 + (1 - core)
-    for k in range(1, n_far):
-        greet(dp, far_peer(k) * 2 + core)
-    for k in range(1, n_dp):
-        greet(dp_peer(k), tp)
-        greet(dp_peer(k), other)
+    for peer in far_peers:
+        greet(dp, peer * 2 + core)
+    for peer in dp_peers:
+        greet(peer, tp)
+        greet(peer, other)
     greet(dp, other)
 
     loads = [
@@ -94,15 +106,17 @@
         pltpu.make_async_copy(weights_hbm, weights, load_sems.at[layers]),
         pltpu.make_async_copy(momentum_hbm, momentum, load_sems.at[layers + 1]),
     ]
-    for load in loads + late:
+    first = pltpu.make_async_copy(factor_hbm, factor, load_sems.at[layers + 2])
+    for load in [first] + loads + late:
         load.start()
 
     left_parts = []
+    first.wait()
     for l in range(layers):
         loads[l].wait()
         left_parts.append(
             lax.dot_general(
-                factor_ref[l].astype(BF16),
+                factor[l].astype(BF16),
                 grads[l],
                 (((1,), (1,)), ((), ())),
                 preferred_element_type=F32,
@@ -118,8 +132,8 @@
     pl.semaphore_wait(barrier, n_far - 1 + 2 * n_dp - 1)
 
     copies_a = [
-        remote(lefts.at[dp], lefts.at[dp], send_sems.at[0], recv_sems.at[0], dp_peer(k), tp)
-        for k in range(1, n_dp)
+        remote(lefts.at[dp], lefts.at[dp], send_sems.at[0], recv_sems.at[0], peer, tp)
+        for peer in dp_peers
     ]
     for copy in copies_a:
         copy.start()
@@ -152,12 +166,8 @@
             )
 
     copies_1 = []
-    for k in range(n_dp):
-        for side in range(2):
-            if k == 0 and side == 0:
-                continue
-            to_core = core if side == 0 else 1 - core
-            to_dp = dp_peer(k)
+    for to_dp in dp_peers + [dp]:
+        for to_core in (core, 1 - core) if to_dp is not dp else (1 - core,):
             copies_1.append(
                 remote(
                     pieces.at[to_dp * 2 + to_core],
@@ -187,9 +197,9 @@
 
     copies_2 = [
         remote(
-            sums.at[far], sums.at[far], send_sems.at[2], recv_sems.at[2], dp, far_peer(k) * 2 + core
-        )
-        for k in range(1, n_far)
+            sums.at[far], sums.at[far], send_sems.at[2], recv_sems.at[2], dp, peer * 2 + core
+        )
+        for peer in far_peers
     ]
     for copy in copies_2:
         copy.start()
@@ -204,7 +214,7 @@
     )
     near.start()
     copies_3 = []
-    for k in range(1, n_dp):
+    for peer in dp_peers:
         for to_tp in (tp, other):
             copies_3.append(
                 remote(
@@ -212,7 +222,7 @@
                     whole.at[group],
                     send_sems.at[4],
                     recv_sems.at[4],
-                    dp_peer(k),
+                    peer,
                     to_tp,
                 )
             )
@@ -257,6 +267,17 @@
     take_bytes(whole.at[pl.ds(0, n_group - 2)], send_sems.at[4])
 
 
+def put_out(a_ref, b_ref, c_ref, a_hbm, b_hbm, c_hbm, sems):
+    moves = [
+        pltpu.make_async_copy(src, dst, sems.at[i])
+        for i, (src, dst) in enumerate(((a_ref, a_hbm), (c_ref, c_hbm), (b_ref, b_hbm)))
+    ]
+    for move in moves:
+        move.start()
+    for move in moves:
+        move.wait()
+
+
 def solution(mesh):
     n_dp = mesh.shape["dp"]
     n_far = mesh.shape["tp"] // 2
@@ -273,14 +294,15 @@
         new_weights, new_basis, new_momentum = pl.pallas_call(
             functools.partial(kernel, n_dp, n_far),
             out_shape=(
-                jax.ShapeDtypeStruct(block, F32),
-                jax.ShapeDtypeStruct(factor.shape, F32),
-                jax.ShapeDtypeStruct(block, F32),
+                pltpu.VMEM(block, F32),
+                pltpu.VMEM(factor.shape, F32),
+                pltpu.VMEM(block, F32),
             ),
-            in_specs=[hbm, vmem, hbm, hbm],
+            in_specs=[hbm] * 4,
             out_specs=(vmem, vmem, vmem),
             scratch_shapes=[
                 pltpu.VMEM(grads.shape, BF16),
+                pltpu.VMEM(factor.shape, F32),
                 pltpu.VMEM(block, F32),
                 pltpu.VMEM(block, F32),
                 pltpu.VMEM((n_dp, layers + half, RANK, LANES), F32),
@@ -289,12 +311,22 @@
                 pltpu.VMEM((n_far,) + tile, F32),
                 pltpu.VMEM((2 * n_dp,) + tile, F32),
                 pltpu.VMEM((layers, rows, 6 * RANK), BF16),
-                pltpu.SemaphoreType.DMA((layers + 2,)),
+                pltpu.SemaphoreType.DMA((layers + 3,)),
                 pltpu.SemaphoreType.DMA((5,)),
                 pltpu.SemaphoreType.DMA((5,)),
             ],
             compiler_params=pltpu.CompilerParams(collective_id=0, has_side_effects=True),
         )(grads, factor, weights_before, momentum)
+        new_weights, new_basis, new_momentum = pl.pallas_call(
+            put_out,
+            out_shape=tuple(
+                jax.ShapeDtypeStruct(v.shape, F32) for v in (new_weights, new_basis, new_momentum)
+            ),
+            in_specs=[vmem] * 3,
+            out_specs=(hbm,) * 3,
+            scratch_shapes=[pltpu.SemaphoreType.DMA((3,))],
+            compiler_params=pltpu.CompilerParams(vmem_limit_bytes=1000000),
+        )(new_weights, new_basis, new_momentum)
         return new_weights, jnp.swapaxes(new_basis, 1, 2), new_momentum
 
     return jax.shard_map(

time: 33.2 us -> 28 us (0.84)
  local copies, waits for them, and re-layouts: 4.11 us -> 0 us
  Pallas kernels: 28.2 us -> 27.2 us
    unnamed x5 -> x0, local copies, waits for them, and re-layouts: 4.11 us -> none
    pallas_call x1 -> x2, Pallas kernels: 28.2 us -> 27.2 us  [the longest x1 26.3 us: step(): pl.pallas_call(functools.partial(kernel, n_dp, n_far), out_shape=(pltpu.V...]
where the time goes in v2:
time: 28 us; the launch traced here: 27.9 us
  Pallas kernels  27.2 us (97%)
  between operations  0.64 us (2%)
    pallas_call x1, Pallas kernels, step(): pl.pallas_call(functools.partial(kernel, n_dp, n_far), out_shape=(pltpu.V...  26.3 us
    pallas_call x1, Pallas kernels, step(): pl.pallas_call(put_out, out_shape=tuple((jax.ShapeDtypeStruct(v.shape, F3...  0.93 us

profile of v2, /device:TPU:1, one launch (start us, length us, event | category | flops | bytes accessed | tf_op | source)
XLA Modules:
  0.0 27.9 jit_solution(72404815181365813)
XLA Ops:
  0.6 26.3 %shard_map.67 = (f32[4,192,96]{2,1,0:T(8,128)S(1)}, f32[4,8,768]{2,1,0:T(8,128)S(1)}, f32[4,192,96]{2,1,0:T(8,128)S(1)}) custom-call(bf16[4,192,768]{2,1,0:T(8,128)(2,1)} %bitcast.3, f32[4,8,768]{2,1,0:T(8,128)} %bitcast.4, f32[4,192,96]{2,1,0:T(8,128)} %weights_hbm.1, f32[4,192,96]{2,1,0:T(8,128)} %momentum_hbm.1), custom_call_target="tpu_custom_call" | custom-call | tf_op jit(solution)/shard_map/pallas_call | solution.py:294
  26.9 0.9 %shard_map.68 = (f32[4,192,96]{2,1,0:T(8,128)}, f32[4,8,768]{2,1,0:T(8,128)}, f32[4,192,96]{2,1,0:T(8,128)}) custom-call(f32[4,192,96]{2,1,0:T(8,128)S(1)} %get-tuple-element.9.a_ref, f32[4,8,768]{2,1,0:T(8,128)S(1)} %get-tuple-element.10.b_ref, f32[4,192,96]{2,1,0:T(8,128)S(1)} %get-tuple-element.11.c_ref), custom_call_target="tpu_custom_call" | custom-call | tf_op jit(solution)/shard_map/pallas_call | solution.py:320
